TPU v7x, 32 devices: a whole 2x2x4 slice. The times are simulated.
32 devices in a mesh: pair: 8 (over z, y), aux: 4 (over x, core).
Axes of the slice: x: 2, y: 2, z: 4, core: 2. Of those that a mesh axis runs over, the one named last changes fastest.
Arguments:
- ints_ac: bfloat16 [192, 512, 4096], P(None, ('pair', 'aux')), may hold values from -0.375 to 0.375
- slot_pair: int32 [192], replicated, may hold values from 0 to 191, each once
- amplitudes: bfloat16 [192, 2, 4096], P(('pair', 'aux')), may hold values from -6 to 6
- ranks: int32 [192], P(('pair', 'aux')), may hold values from 16 to 64
- pair_occ: int32 [192, 2], P(('pair', 'aux')), may hold values from 0 to 47
- pno_energy: float32 [192, 64], P(('pair', 'aux')), may hold values from 0.2 to 3
- occ_energy: float32 [48], replicated, may hold values from -2 to -0.3
Outputs:
- ext_residual: float32 [192, 2, 4096], P(('pair', 'aux'))
- new_amplitudes: bfloat16 [192, 2, 4096], P(('pair', 'aux'))
Inputs may be any that keep to these rules, and one draw needn't show every extreme that they name: `slot_pair`: a permutation of the pairs. Entries a >= ranks[s] of a slot's blocks are padding.
All inputs are finite; a program needn't handle non-finite values.
Results may differ from a plain program's by a relative error of at most 0.0039.
Values may be sent and summed in bfloat16 or wider, within the bound.
A program may use at most 128 MiB of HBM per device.

v0:
```python
import jax
import jax.numpy as jnp
from jax import lax
from jax.experimental import pallas as pl
from jax.experimental.pallas import tpu as pltpu
from jax.sharding import PartitionSpec as P

GROUP = 8


def exchange_kernel(group, width, order_ref, *refs):
    blocks, amps_ref, out_ref, rows_ref = refs[:group], refs[group], refs[group + 1], refs[group + 2]
    lanes = 2 * width
    aux = blocks[0].shape[1]
    chunks = width * width // lanes
    half_t = lax.broadcasted_iota(jnp.int32, (width, lanes), 1) < width
    half_b = lax.broadcasted_iota(jnp.int32, (chunks, lanes), 1) < width
    for slot in range(group):
        block = blocks[slot]
        for chunk in range(chunks):
            rows_ref[slot, pl.ds(chunk * aux, aux), :] = block[
                0, :, pl.ds(chunk * lanes, lanes)
            ].astype(jnp.float32)
        pieces = []
        for pair in range(aux // 2):
            first = rows_ref[slot, pl.ds(2 * pair, chunks, stride=aux), :]
            second = rows_ref[slot, pl.ds(2 * pair + 1, chunks, stride=aux), :]
            even = jnp.where(half_b, first, pltpu.roll(second, width, 1))
            odd = jnp.where(half_b, pltpu.roll(first, width, 1), second)
            pieces.append(jnp.concatenate([even, odd], axis=0).astype(jnp.bfloat16))
        stacked = jnp.concatenate(pieces, axis=0)
        amps = amps_ref[slot].astype(jnp.float32)
        turned = pltpu.roll(amps, width, 1)
        none = jnp.zeros_like(amps)
        weights = jnp.concatenate(
            [
                jnp.concatenate([jnp.where(half_t, amps, none), jnp.where(half_t, none, turned)], axis=0),
                jnp.concatenate([jnp.where(half_t, turned, none), jnp.where(half_t, none, amps)], axis=0),
            ],
            axis=1,
        ).astype(jnp.bfloat16)
        inner = jnp.dot(stacked, weights, preferred_element_type=jnp.float32).astype(jnp.bfloat16)
        left = jnp.concatenate(pieces, axis=1)
        right = jnp.concatenate(
            [
                jnp.concatenate(
                    [
                        inner[pair * width : (pair + 1) * width, k * lanes : (k + 1) * lanes]
                        for pair in range(aux // 2)
                    ],
                    axis=1,
                )
                for k in range(2)
            ],
            axis=0,
        )
        out_ref[slot] = lax.dot_general(
            left, right, (((1,), (1,)), ((), ())), preferred_element_type=jnp.float32
        ).astype(out_ref.dtype)


def partials(ints_ac, slot_pair, amps):
    count, width, lanes = amps.shape
    aux = ints_ac.shape[1]
    group = max(g for g in range(1, GROUP + 1) if count % g == 0)

    def block_map(offset):
        return lambda step, order: (order[step * group + offset], 0, 0)

    return pl.pallas_call(
        lambda *refs: exchange_kernel(group, width, *refs),
        grid_spec=pltpu.PrefetchScalarGridSpec(
            num_scalar_prefetch=1,
            grid=(count // group,),
            in_specs=[
                pl.BlockSpec((1, aux, width * width), block_map(offset)) for offset in range(group)
            ]
            + [pl.BlockSpec((group, width, lanes), lambda step, order: (step, 0, 0))],
            out_specs=pl.BlockSpec((group, width, lanes), lambda step, order: (step, 0, 0)),
            scratch_shapes=[pltpu.VMEM((group, aux * width // 2, lanes), jnp.float32)],
        ),
        out_shape=jax.ShapeDtypeStruct((count, width, lanes), jnp.bfloat16),
        cost_estimate=pl.CostEstimate(
            flops=8 * count * aux * width**3,
            bytes_accessed=ints_ac.size * 2 + amps.size * 4,
            transcendentals=0,
        ),
        name="exchange",
    )(slot_pair, *([ints_ac] * group), amps)


def body(ints_ac, slot_pair, amplitudes, ranks, pair_occ, pno_energy, occ_energy):
    width = pno_energy.shape[1]
    local = amplitudes.shape[0]
    positions = jnp.arange(width, dtype=jnp.int32)
    masks = (positions[None, :] < ranks[:, None]).astype(jnp.float32)
    square = masks[:, :, None] * masks[:, None, :]
    masked_t = amplitudes.astype(jnp.float32).reshape(local, 2, width, width) * square[:, None]
    own = masked_t.astype(jnp.bfloat16).transpose(0, 2, 1, 3).reshape(local, width, 2 * width)
    every = lax.all_gather(own, ("pair", "aux"), axis=0, tiled=True)
    out = partials(ints_ac, slot_pair, every)
    parts = lax.all_to_all(out, ("pair", "aux"), 0, 0, tiled=True)
    parts = parts.reshape(-1, local, width, 2 * width)
    summed = parts.astype(jnp.float32).sum(axis=0)
    source = (positions % 2) * (width // 2) + positions // 2
    place = (positions[:, None] == source[None, :]).astype(jnp.float32)
    split = summed.reshape(local, width, 2, width)
    residual = jnp.einsum(
        "jykx,xa,yb->jkab", split, place, place, precision=lax.Precision.HIGHEST
    )
    residual = residual * square[:, None]
    onehot = (
        pair_occ[:, :, None] == jnp.arange(occ_energy.shape[0], dtype=jnp.int32)[None, None, :]
    ).astype(jnp.float32)
    occ_pair = jnp.einsum("jko,o->jk", onehot, occ_energy, precision=lax.Precision.HIGHEST)
    denom = (
        pno_energy[:, :, None]
        + pno_energy[:, None, :]
        - (occ_pair[:, 0] + occ_pair[:, 1])[:, None, None]
    )
    updated = (masked_t - residual / denom[:, None]) * square[:, None]
    return (
        residual.reshape(local, 2, width * width),
        updated.reshape(local, 2, width * width).astype(jnp.bfloat16),
    )


def solution(mesh):
    placed = (
        P(None, ("pair", "aux"), None),
        P(),
        P(("pair", "aux"), None, None),
        P(("pair", "aux")),
        P(("pair", "aux"), None),
        P(("pair", "aux"), None),
        P(),
    )
    return jax.shard_map(
        body,
        mesh=mesh,
        in_specs=placed,
        out_specs=(P(("pair", "aux"), None, None), P(("pair", "aux"), None, None)),
        check_vma=False,
    )
```

profile of v0, /device:TPU:0, one launch (start us, length us, event | category | flops | bytes accessed | tf_op | source)
XLA Modules:
  0.0 211.1 jit_solution(4877332694024305031)
XLA Ops:
  7.2 0.0 copy-start
  7.2 0.0 all-gather.2.cloned.1.call-start
  7.2 1.0 reshape.106
  8.3 0.8 copy.18
  9.0 0.1 iota_compare_fusion.1
  9.1 0.0 copy-done
  9.1 0.1 fusion.10
  9.3 0.8 fusion.12
  10.1 1.6 add_subtract_fusion
  11.6 0.0 copy-start.1
  11.6 0.7 copy-done.1
  12.4 0.2 copy.15
  12.6 0.8 reshape.102
  13.4 0.0 all-gather.2.cloned.1.call-update
  13.4 62.0 %all-gather.2.cloned.1.call-done.refs_9_ = bf16[192,64,128]{2,1,0:T(8,128)(2,1)} async-done(((bf16[6,64,128]{2,1,0:T(8,128)(2,1)}), bf16[192,64,128]{2,1,0:T(8,128)(2,1)}) %all-gather.2.cloned.1.call-update) | async-done | bytes 3145744 | tf_op jit(solution)/shard_map/all_gather | solution.py:100
  75.4 47.9 %exchange.1 = bf16[192,64,128]{2,1,0:T(8,128)(2,1)} custom-call(s32[192]{0:T(256)} %refs_0_.1, bf16[192,16,4096]{2,1,0:T(8,128)(2,1)} %refs_8_.1, bf16[192,16,4096]{2,1,0:T(8,128)(2,1)} %refs_8_.1, bf16[192,16,4096]{2,1,0:T(8,128)(2,1)} %refs_8_.1, bf16[192,16,4096]{2,1,0:T(8,128)(2,1)} %refs_8_.1, bf16[192,16,4096]{2,1,0:T(8,128)(2,1)} %refs_8_.1, ...), custom_call_target="tpu_custom_call" | custom-call | flops 6442450944 | bytes 31457280 | tf_op jit(solution)/shard_map/exchange/pallas_call | solution.py:70
  123.3 3.3 %all-to-all-start = ((bf16[192,64,128]{2,1,0:T(8,128)(2,1)}), bf16[192,64,128]{2,1,0:T(8,128)(2,1)S(1)}, u32[]{:S(2)}, u32[]{:S(2)}) async-start(bf16[192,64,128]{2,1,0:T(8,128)(2,1)} %exchange.1), calls=%async_computation | async-start | bytes 6291456 | tf_op jit(solution)/shard_map/all_to_all | solution.py:102
  126.6 71.3 %all-to-all-done = bf16[192,64,128]{2,1,0:T(8,128)(2,1)S(1)} async-done(((bf16[192,64,128]{2,1,0:T(8,128)(2,1)}), bf16[192,64,128]{2,1,0:T(8,128)(2,1)S(1)}, u32[]{:S(2)}, u32[]{:S(2)}) %all-to-all-start) | async-done | bytes 3145760 | tf_op jit(solution)/shard_map/all_to_all | solution.py:102
  197.9 1.3 convert_reduce_fusion
  199.2 1.2 reshape.103
  200.4 0.7 fusion.1
  201.1 1.4 multiply_convert_fusion
  202.5 0.9 reshape.104
  203.4 0.8 convert_element_type.34
  (3 shorter events, 0.1 us)
Async XLA Ops:
  7.2 2.0 copy-start
  7.2 68.2 %all-gather.2.cloned.1.call-start = ((), (), s32[]{:S(2)}) async-start(), calls=%async_computation.1 | async-start | bytes 3244032 | tf_op jit(solution)/shard_map/all_gather | solution.py:100
  11.6 0.7 copy-start.1
  123.3 74.7 %all-to-all-start = ((bf16[192,64,128]{2,1,0:T(8,128)(2,1)}), bf16[192,64,128]{2,1,0:T(8,128)(2,1)S(1)}, u32[]{:S(2)}, u32[]{:S(2)}) async-start(bf16[192,64,128]{2,1,0:T(8,128)(2,1)} %exchange.1), calls=%async_computation | async-start | bytes 6291456 | tf_op jit(solution)/shard_map/all_to_all | solution.py:102
Sparse Core Ops, SparseCore 0:
  13.5 61.7 all-gather.1
where the time goes:
time: 211 us
  waiting for transfers between devices  133 us (63%)
  Pallas kernels  47.9 us (23%)
  between operations  14.1 us (7%)
  local copies, waits for them, and re-layouts  6.38 us (3%)
  other arithmetic  3.82 us (2%)
  starting transfers between devices  3.37 us (2%)
  matrix products  2.2 us (1%)
    all_to_all x1, waiting for transfers between devices, body(): parts = lax.all_to_all(out, ('pair', 'aux'), 0, 0, tiled=True)  71.3 us
    all_gather x1, waiting for transfers between devices, body(): every = lax.all_gather(own, ('pair', 'aux'), axis=0, tiled=True)  62 us
    pallas_call x1, Pallas kernels, partials(): pl.pallas_call(lambda *refs: exchange_kernel(group, width, *refs), grid_s...  47.9 us
  transfers between devices with their start and end apart: 2, of which 2 were waited for; matrix products, arithmetic and copies ran while one was open for 0% of the time, Pallas kernels for 0%

commit v1 on v0

--- a/solution.py
+++ b/solution.py
@@ -1,3 +1,5 @@
+import functools
+
 import jax
 import jax.numpy as jnp
 from jax import lax
@@ -89,7 +91,256 @@
     )(slot_pair, *([ints_ac] * group), amps)
 
 
-def body(ints_ac, slot_pair, amplitudes, ranks, pair_occ, pno_energy, occ_energy):
+def layout_of(pairs, aux):
+    side = aux // 2
+    if pairs % side:
+        side = 1
+    return pairs // side, side, aux // side // 2
+
+
+class Place:
+    def __init__(self, pairs, aux):
+        self.deep, self.side, _ = layout_of(pairs, aux)
+        pair, lane = lax.axis_index("pair"), lax.axis_index("aux")
+        self.z, self.y = pair // self.side, pair % self.side
+        self.x, self.core = lane // 2, lane % 2
+
+    def spot(self, dz, i, j):
+        z = (self.z + dz) % self.deep
+        y = (self.y + i * (1 - self.core) + j * self.core) % self.side
+        x = (self.x + j * (1 - self.core) + i * self.core) % self.side
+        return z, y, x
+
+    def block(self, dz, i, j):
+        z, y, x = self.spot(dz, i, j)
+        return ((z * self.side + y) * self.side + x) * 2 + self.core
+
+    def device(self, dz, i, j):
+        z, y, x = self.spot(dz, i, j)
+        return {"pair": z * self.side + y, "aux": x * 2 + self.core}
+
+    def partner(self):
+        return {"pair": self.z * self.side + self.y, "aux": self.x * 2 + 1 - self.core}
+
+    def peers(self):
+        found = [self.device(dz, 0, 0) for dz in range(1, self.deep)]
+        found += [self.device(0, i, 0) for i in range(1, self.side)]
+        found += [self.device(0, 0, j) for j in range(1, self.side)]
+        return found + [self.partner()]
+
+    def greet(self):
+        barrier = pltpu.get_barrier_semaphore()
+        peers = self.peers()
+        for peer in peers:
+            pl.semaphore_signal(barrier, inc=1, device_id=peer, device_id_type=pl.DeviceIdType.MESH)
+        pl.semaphore_wait(barrier, len(peers))
+
+
+class Sender:
+    def __init__(self, sems):
+        self.sems, self.started = sems, []
+
+    def send(self, source, target, arrival, device):
+        copy = pltpu.make_async_remote_copy(
+            src_ref=source,
+            dst_ref=target,
+            send_sem=self.sems.at[len(self.started)],
+            recv_sem=arrival,
+            device_id=device,
+            device_id_type=pl.DeviceIdType.MESH,
+        )
+        copy.start()
+        self.started.append(copy)
+
+    def arrived(self, target, arrival, device):
+        pltpu.make_async_remote_copy(
+            src_ref=target,
+            dst_ref=target,
+            send_sem=self.sems.at[0],
+            recv_sem=arrival,
+            device_id=device,
+            device_id_type=pl.DeviceIdType.MESH,
+        ).wait_recv()
+
+    def finish(self):
+        for copy in self.started:
+            copy.wait_send()
+
+
+def gather_kernel(pairs, aux, own_ref, out_ref, send_sem, recv_sem, local_sem):
+    here = Place(pairs, aux)
+    deep, side = here.deep, here.side
+    out = Sender(send_sem)
+    keep = pltpu.make_async_copy(own_ref, out_ref.at[here.block(0, 0, 0)], local_sem)
+    keep.start()
+    here.greet()
+
+    def forward(dz, i, j, source):
+        block = here.block(dz, i, j)
+        target, arrival = out_ref.at[block], recv_sem.at[block]
+        if j == 0:
+            for step in range(1, side):
+                out.send(source, target, arrival, here.device(0, 0, step))
+        if i == 0 and j == 0:
+            for step in range(1, side):
+                out.send(source, target, arrival, here.device(0, step, 0))
+        if dz == 0 and i == 0 and j == 0:
+            for step in range(1, deep):
+                out.send(source, target, arrival, here.device(step, 0, 0))
+        out.send(source, target, arrival, here.partner())
+
+    def pass_on(dz, i, j):
+        block = here.block(dz, i, j)
+        out.arrived(out_ref.at[block], recv_sem.at[block], here.partner())
+        forward(dz, i, j, out_ref.at[block])
+
+    forward(0, 0, 0, own_ref)
+    for dz in range(deep):
+        if dz:
+            pass_on(dz, 0, 0)
+        for i in range(1, side):
+            pass_on(dz, i, 0)
+    for dz in range(deep):
+        for i in range(side):
+            for j in range(1, side):
+                pass_on(dz, i, j)
+    for dz in range(deep):
+        for i in range(side):
+            for j in range(side):
+                z, y, x = here.spot(dz, i, j)
+                block = ((z * side + y) * side + x) * 2 + 1 - here.core
+                out.arrived(out_ref.at[block], recv_sem.at[block], here.partner())
+    out.finish()
+    keep.wait()
+
+
+def gather(own, pairs, aux):
+    blocks = pairs * aux
+    return pl.pallas_call(
+        functools.partial(gather_kernel, pairs, aux),
+        in_specs=[pl.BlockSpec(memory_space=pltpu.VMEM)],
+        out_specs=pl.BlockSpec(memory_space=pltpu.VMEM),
+        out_shape=jax.ShapeDtypeStruct((blocks,) + own.shape, own.dtype),
+        scratch_shapes=[
+            pltpu.SemaphoreType.DMA((blocks,)),
+            pltpu.SemaphoreType.DMA((blocks,)),
+            pltpu.SemaphoreType.DMA,
+        ],
+        compiler_params=pltpu.CompilerParams(collective_id=0, has_side_effects=True, vmem_limit_bytes=48 << 20),
+        name="gather",
+    )(own)
+
+
+def scatter_kernel(
+    pairs, aux, part_ref, out_ref, held, mate, third, second, last, third_out, second_out, last_out,
+    send_sem, mate_sem, third_sem, second_sem, last_sem,
+):
+    here = Place(pairs, aux)
+    deep, side = here.deep, here.side
+    out = Sender(send_sem)
+    here.greet()
+    order = [*range(1, deep), 0]
+    inner = [*range(1, side), 0]
+
+    def spatial(dz, i, j):
+        z, y, x = here.spot(dz, i, j)
+        return (z * side + y) * side + x
+
+    for group in (range(1, side), range(1)):
+        for dz in order:
+            for j in inner:
+                for i in group:
+                    place = spatial(dz, i, j)
+                    out.send(part_ref.at[place * 2 + 1 - here.core], mate.at[place], mate_sem.at[place], here.partner())
+
+    def joined(dz, i, j):
+        place = spatial(dz, i, j)
+        out.arrived(mate.at[place], mate_sem.at[place], here.partner())
+        return part_ref[place * 2 + here.core].astype(jnp.float32) + mate[place].astype(jnp.float32)
+
+    for dz in order:
+        for i in inner:
+            for j in range(1, side):
+                slot = (dz * side + i) * (side - 1) + j - 1
+                third_out[slot] = joined(dz, i, j).astype(third_out.dtype)
+                out.send(third_out.at[slot], third.at[slot], third_sem.at[slot], here.device(0, 0, j))
+    for dz in order:
+        for i in inner:
+            held[dz * side + i] = joined(dz, i, 0)
+
+    def sum_third(dz, i):
+        total = held[dz * side + i]
+        for j in range(1, side):
+            slot = (dz * side + i) * (side - 1) + j - 1
+            out.arrived(third.at[slot], third_sem.at[slot], here.partner())
+            total = total + third[slot].astype(jnp.float32)
+        return total
+
+    def sum_second(dz):
+        total = held[dz * side]
+        for i in range(1, side):
+            slot = dz * (side - 1) + i - 1
+            out.arrived(second.at[slot], second_sem.at[slot], here.partner())
+            total = total + second[slot].astype(jnp.float32)
+        return total
+
+    def send_last(dz):
+        last_out[dz - 1] = sum_second(dz).astype(last_out.dtype)
+        out.send(last_out.at[dz - 1], last.at[dz - 1], last_sem.at[dz - 1], here.device(dz, 0, 0))
+
+    for turn, dz in enumerate(order):
+        for i in range(1, side):
+            slot = dz * (side - 1) + i - 1
+            second_out[slot] = sum_third(dz, i).astype(second_out.dtype)
+            out.send(second_out.at[slot], second.at[slot], second_sem.at[slot], here.device(0, i, 0))
+        held[dz * side] = sum_third(dz, 0)
+        if turn:
+            send_last(order[turn - 1])
+    total = sum_second(0)
+    for dz in range(1, deep):
+        out.arrived(last.at[dz - 1], last_sem.at[dz - 1], here.partner())
+        total = total + last[dz - 1].astype(jnp.float32)
+    out_ref[...] = total
+    out.finish()
+
+
+def scatter(parts, pairs, aux):
+    blocks = pairs * aux
+    deep, side, _ = layout_of(pairs, aux)
+    shape, kind = parts.shape[1:], parts.dtype
+    counts = {
+        "mate": blocks // 2,
+        "third": deep * side * (side - 1),
+        "second": deep * (side - 1),
+        "last": deep - 1,
+    }
+    thirds, seconds, lasts = (max(1, counts[name]) for name in ("third", "second", "last"))
+    return pl.pallas_call(
+        functools.partial(scatter_kernel, pairs, aux),
+        in_specs=[pl.BlockSpec(memory_space=pltpu.VMEM)],
+        out_specs=pl.BlockSpec(memory_space=pltpu.VMEM),
+        out_shape=jax.ShapeDtypeStruct(shape, jnp.float32),
+        scratch_shapes=[
+            pltpu.VMEM((deep * side,) + shape, jnp.float32),
+            pltpu.VMEM((counts["mate"],) + shape, kind),
+            pltpu.VMEM((thirds,) + shape, kind),
+            pltpu.VMEM((seconds,) + shape, kind),
+            pltpu.VMEM((lasts,) + shape, kind),
+            pltpu.VMEM((thirds,) + shape, kind),
+            pltpu.VMEM((seconds,) + shape, kind),
+            pltpu.VMEM((lasts,) + shape, kind),
+            pltpu.SemaphoreType.DMA((blocks,)),
+            pltpu.SemaphoreType.DMA((counts["mate"],)),
+            pltpu.SemaphoreType.DMA((thirds,)),
+            pltpu.SemaphoreType.DMA((seconds,)),
+            pltpu.SemaphoreType.DMA((lasts,)),
+        ],
+        compiler_params=pltpu.CompilerParams(collective_id=1, has_side_effects=True, vmem_limit_bytes=56 << 20),
+        name="scatter",
+    )(parts)
+
+
+def body(pairs, aux, ints_ac, slot_pair, amplitudes, ranks, pair_occ, pno_energy, occ_energy):
     width = pno_energy.shape[1]
     local = amplitudes.shape[0]
     positions = jnp.arange(width, dtype=jnp.int32)
@@ -97,11 +348,9 @@
     square = masks[:, :, None] * masks[:, None, :]
     masked_t = amplitudes.astype(jnp.float32).reshape(local, 2, width, width) * square[:, None]
     own = masked_t.astype(jnp.bfloat16).transpose(0, 2, 1, 3).reshape(local, width, 2 * width)
-    every = lax.all_gather(own, ("pair", "aux"), axis=0, tiled=True)
+    every = gather(own, pairs, aux).reshape(-1, width, 2 * width)
     out = partials(ints_ac, slot_pair, every)
-    parts = lax.all_to_all(out, ("pair", "aux"), 0, 0, tiled=True)
-    parts = parts.reshape(-1, local, width, 2 * width)
-    summed = parts.astype(jnp.float32).sum(axis=0)
+    summed = scatter(out.reshape(-1, local, width, 2 * width), pairs, aux)
     source = (positions % 2) * (width // 2) + positions // 2
     place = (positions[:, None] == source[None, :]).astype(jnp.float32)
     split = summed.reshape(local, width, 2, width)
@@ -136,7 +385,7 @@
         P(),
     )
     return jax.shard_map(
-        body,
+        functools.partial(body, mesh.shape["pair"], mesh.shape["aux"]),
         mesh=mesh,
         in_specs=placed,
         out_specs=(P(("pair", "aux"), None, None), P(("pair", "aux"), None, None)),

time: 211 us -> 115 us (0.55)
  waiting for transfers between devices: 133 us -> 0 us
  Pallas kernels: 47.9 us -> 105 us
  between operations: 14.1 us -> 0.73 us
  starting transfers between devices: 3.37 us -> 0 us
    all_to_all x1 -> x0, waiting for transfers between devices: 71.3 us -> none  [body(): parts = lax.all_to_all(out, ('pair', 'aux'), 0, 0, tiled=True)]
    all_gather x1 -> x0, waiting for transfers between devices: 62 us -> none  [body(): every = lax.all_gather(own, ('pair', 'aux'), axis=0, tiled=True)]
    pallas_call x0 -> x2, Pallas kernels: none -> 56.8 us  [the longest x1 29.9 us: gather(): pl.pallas_call(functools.partial(gather_kernel, pairs, aux), in_specs=[pl...]
    all_to_all x1 -> x0, starting transfers between devices: 3.33 us -> none  [body(): parts = lax.all_to_all(out, ('pair', 'aux'), 0, 0, tiled=True)]
  transfers between devices with their start and end apart: 2 -> 0, of which waited for: 2 -> 0; matrix products, arithmetic and copies ran while one was open for 0% -> 0% of each run, Pallas kernels for 0% -> 0%
where the time goes in v1:
time: 115 us
  Pallas kernels  105 us (91%)
  local copies, waits for them, and re-layouts  6.63 us (6%)
  other arithmetic  1.85 us (2%)
    pallas_call x1, Pallas kernels, partials(): pl.pallas_call(lambda *refs: exchange_kernel(group, width, *refs), grid_s...  47.9 us
    pallas_call x1, Pallas kernels, gather(): pl.pallas_call(functools.partial(gather_kernel, pairs, aux), in_specs=[pl...  29.9 us
    pallas_call x1, Pallas kernels, scatter(): pl.pallas_call(functools.partial(scatter_kernel, pairs, aux), in_specs=[p...  26.9 us
    unnamed x5, local copies, waits for them, and re-layouts  2.43 us

profile of v1, /device:TPU:0, one launch (start us, length us, event | category | flops | bytes accessed | tf_op | source)
XLA Modules:
  0.0 114.8 jit_solution(10926810492342058601)
XLA Ops:
  0.6 0.0 copy-start
  0.6 1.1 reshape.111
  1.7 0.8 copy.10
  2.5 0.1 iota_compare_fusion.1
  2.5 0.0 copy-done
  2.5 0.1 fusion.8
  2.7 0.8 fusion.10
  3.5 0.9 add_subtract_fusion
  4.5 0.2 copy.9
  4.7 0.1 reshape.105.own_ref
  4.8 29.9 %gather.1 = bf16[32,6,64,128]{3,2,1,0:T(8,128)(2,1)S(1)} custom-call(bf16[6,64,128]{2,1,0:T(8,128)(2,1)S(1)} %reshape.105.own_ref), custom_call_target="tpu_custom_call" | custom-call | tf_op jit(solution)/shard_map/gather/pallas_call | solution.py:219
  34.7 0.0 copy-start.1
  34.8 1.7 %copy-done.1 = bf16[32,6,64,128]{3,2,1,0:T(8,128)(2,1)} copy-done((bf16[32,6,64,128]{3,2,1,0:T(8,128)(2,1)}, bf16[32,6,64,128]{3,2,1,0:T(8,128)(2,1)S(1)}, u32[]{:S(2)}) %copy-start.1) | copy-done | bytes 3145752
  36.4 47.9 %exchange.1 = bf16[192,64,128]{2,1,0:T(8,128)(2,1)} custom-call(s32[192]{0:T(256)} %refs_0_.1, bf16[192,16,4096]{2,1,0:T(8,128)(2,1)} %refs_8_.1, bf16[192,16,4096]{2,1,0:T(8,128)(2,1)} %refs_8_.1, bf16[192,16,4096]{2,1,0:T(8,128)(2,1)} %refs_8_.1, bf16[192,16,4096]{2,1,0:T(8,128)(2,1)} %refs_8_.1, bf16[192,16,4096]{2,1,0:T(8,128)(2,1)} %refs_8_.1, ...), custom_call_target="tpu_custom_call" | custom-call | flops 6442450944 | bytes 31457280 | tf_op jit(solution)/shard_map/exchange/pallas_call | solution.py:72
  84.3 26.9 %scatter.1 = f32[6,64,128]{2,1,0:T(8,128)} custom-call(bf16[32,6,64,128]{3,2,1,0:T(8,128)(2,1)} %bitcast.32), custom_call_target="tpu_custom_call" | custom-call | tf_op jit(solution)/shard_map/scatter/pallas_call | solution.py:318
  111.2 1.1 copy.15
  112.3 0.4 fusion.4
  112.7 0.3 multiply_convert_fusion
  113.1 0.9 reshape.109
  113.9 0.8 convert_element_type.26
  (3 shorter events, 0.1 us)
Async XLA Ops:
  0.6 1.9 %copy-start = (f32[48]{0:T(128)S(1)}, f32[48]{0:T(128)}, u32[]{:S(2)}) copy-start(f32[48]{0:T(128)} %param.13) | copy-start | bytes 580
  34.7 1.7 %copy-start.1 = (bf16[32,6,64,128]{3,2,1,0:T(8,128)(2,1)}, bf16[32,6,64,128]{3,2,1,0:T(8,128)(2,1)S(1)}, u32[]{:S(2)}) copy-start(bf16[32,6,64,128]{3,2,1,0:T(8,128)(2,1)S(1)} %gather.1) | copy-start | bytes 9437188

commit v2 on v0

v2 whole, which is shorter than its diff:
```python
import functools

import jax
import jax.numpy as jnp
from jax import lax
from jax.experimental import pallas as pl
from jax.experimental.pallas import tpu as pltpu
from jax.sharding import PartitionSpec as P

CHUNKS = 8


def exchange(load, amps, rows_ref):
    width, lanes = amps.shape
    chunks = width * width // lanes
    aux = rows_ref.shape[0] // chunks
    half_t = lax.broadcasted_iota(jnp.int32, (width, lanes), 1) < width
    half_b = lax.broadcasted_iota(jnp.int32, (chunks, lanes), 1) < width
    for chunk in range(chunks):
        rows_ref[pl.ds(chunk * aux, aux), :] = load(chunk).astype(jnp.float32)
    pieces = []
    for pair in range(aux // 2):
        first = rows_ref[pl.ds(2 * pair, chunks, stride=aux), :]
        second = rows_ref[pl.ds(2 * pair + 1, chunks, stride=aux), :]
        crossed = pltpu.roll(jnp.where(half_b, second, first), width, 1)
        even = jnp.where(half_b, first, crossed)
        odd = jnp.where(half_b, crossed, second)
        pieces.append(jnp.concatenate([even, odd], axis=0).astype(jnp.bfloat16))
    stacked = jnp.concatenate(pieces, axis=0)
    amps = amps.astype(jnp.float32)
    turned = pltpu.roll(amps, width, 1)
    none = jnp.zeros_like(amps)
    weights = jnp.concatenate(
        [
            jnp.concatenate([jnp.where(half_t, amps, none), jnp.where(half_t, none, turned)], axis=0),
            jnp.concatenate([jnp.where(half_t, turned, none), jnp.where(half_t, none, amps)], axis=0),
        ],
        axis=1,
    ).astype(jnp.bfloat16)
    inner = jnp.dot(stacked, weights, preferred_element_type=jnp.float32).astype(jnp.bfloat16)
    left = jnp.concatenate(pieces, axis=1)
    right = jnp.concatenate(
        [
            jnp.concatenate(
                [
                    inner[pair * width : (pair + 1) * width, k * lanes : (k + 1) * lanes]
                    for pair in range(aux // 2)
                ],
                axis=1,
            )
            for k in range(2)
        ],
        axis=0,
    )
    return lax.dot_general(left, right, (((1,), (1,)), ((), ())), preferred_element_type=jnp.float32)


def layout_of(pairs, aux):
    side = aux // 2
    if pairs % side:
        side = 1
    return pairs // side, side, aux // side // 2


class Place:
    def __init__(self, pairs, aux):
        self.deep, self.side, _ = layout_of(pairs, aux)
        pair, lane = lax.axis_index("pair"), lax.axis_index("aux")
        self.z, self.y = pair // self.side, pair % self.side
        self.x, self.core = lane // 2, lane % 2

    def spot(self, dz, i, j):
        z = (self.z + dz) % self.deep
        y = (self.y + i * (1 - self.core) + j * self.core) % self.side
        x = (self.x + j * (1 - self.core) + i * self.core) % self.side
        return z, y, x

    def block(self, dz, i, j):
        z, y, x = self.spot(dz, i, j)
        return ((z * self.side + y) * self.side + x) * 2 + self.core

    def mirror(self, dz, i, j):
        z, y, x = self.spot(dz, j, i)
        return ((z * self.side + y) * self.side + x) * 2 + 1 - self.core

    def device(self, dz, i, j):
        z, y, x = self.spot(dz, i, j)
        return {"pair": z * self.side + y, "aux": x * 2 + self.core}

    def partner(self):
        return {"pair": self.z * self.side + self.y, "aux": self.x * 2 + 1 - self.core}

    def peers(self):
        found = [self.device(dz, 0, 0) for dz in range(1, self.deep)]
        found += [self.device(0, i, 0) for i in range(1, self.side)]
        found += [self.device(0, 0, j) for j in range(1, self.side)]
        return found + [self.partner()]

    def greet(self):
        barrier = pltpu.get_barrier_semaphore()
        peers = self.peers()
        for peer in peers:
            pl.semaphore_signal(barrier, inc=1, device_id=peer, device_id_type=pl.DeviceIdType.MESH)
        pl.semaphore_wait(barrier, len(peers))


def copy_to(source, target, sent, arrival, device):
    return pltpu.make_async_remote_copy(
        src_ref=source,
        dst_ref=target,
        send_sem=sent,
        recv_sem=arrival,
        device_id=device,
        device_id_type=pl.DeviceIdType.MESH,
    )


def residual_kernel(
    pairs, aux, order_ref, ints_ref, own_ref, out_ref,
    ints, amps, rows, fresh, given, mate, held, third, third_out, second, second_out, last, last_out,
    ints_sem, keep_sem, recv_sem, fan_sem, hop3_sem, hop2_sem, hopz_sem,
    given_sem, mate_sem, third_sent, third_sem, second_sent, second_sem, last_sent, last_sem,
):
    here = Place(pairs, aux)
    deep, side = here.deep, here.side
    local = own_ref.shape[0]
    lanes = own_ref.shape[2]
    partner = here.partner()
    square = side * side
    count = ints.shape[0]
    each = count // CHUNKS

    def loads():
        for part in range(CHUNKS):
            span = pl.ds(part * each, each)
            yield pltpu.make_async_copy(ints_ref.at[span], ints.at[span], ints_sem.at[part])

    for load in loads():
        load.start()
    keep = pltpu.make_async_copy(own_ref, amps.at[here.block(0, 0, 0)], keep_sem)
    keep.start()
    here.greet()

    def forward(dz, i, j, source=None, to_third=False, to_second=False, to_deep=False):
        block = here.block(dz, i, j)
        target, arrival = amps.at[block], recv_sem.at[block]
        source = target if source is None else source
        family = (dz * side + i) * side + j
        if to_third:
            for step in range(1, side):
                sent = hop3_sem.at[(dz * side + i) * (side - 1) + step - 1]
                copy_to(source, target, sent, arrival, here.device(0, 0, step)).start()
        if to_second:
            for step in range(1, side):
                sent = hop2_sem.at[dz * (side - 1) + step - 1]
                copy_to(source, target, sent, arrival, here.device(0, step, 0)).start()
        if to_deep:
            for step in range(deep - 1, 0, -1):
                copy_to(source, target, hopz_sem.at[step - 1], arrival, here.device(step, 0, 0)).start()
        copy_to(source, target, fan_sem.at[family], arrival, partner).start()

    def arrived(block):
        copy_to(amps.at[block], amps.at[block], fan_sem.at[0], recv_sem.at[block], partner).wait_recv()

    def pass_on(dz, i, j, **where):
        arrived(here.block(dz, i, j))
        forward(dz, i, j, **where)

    forward(0, 0, 0, own_ref, to_third=True, to_second=True, to_deep=True)
    for i in range(1, side):
        pass_on(0, i, 0, to_third=True)
    pass_on(1, 0, 0, to_third=True, to_second=True)
    for i in range(1, side):
        pass_on(1, i, 0, to_third=True)
    for dz in range(2, deep):
        pass_on(dz, 0, 0, to_third=True, to_second=True)
    for i in range(side):
        for j in range(1, side):
            pass_on(1, i, j)
    keep.wait()
    for load in loads():
        load.wait()

    def compute(block, store):
        for slot in range(local):
            pair = order_ref[block * local + slot]
            store(slot, exchange(
                lambda chunk: ints[pair, :, pl.ds(chunk * lanes, lanes)], amps[block, slot], rows.at[slot]
            ))

    def as_float(value):
        return value.astype(jnp.float32)

    def take(target, arrival):
        copy_to(target, target, given_sem.at[0], arrival, partner).wait_recv()
        return as_float(target[...])

    def third_slot(dz, i, j):
        return (dz * side + i) * (side - 1) + j - 1

    def sum_third(dz, i):
        total = held[dz * side + i]
        for j in range(1, side):
            slot = third_slot(dz, i, j)
            total = total + take(third.at[slot], third_sem.at[slot])
        return total

    def sum_second(dz):
        total = held[dz * side]
        for i in range(1, side):
            slot = dz * (side - 1) + i - 1
            total = total + take(second.at[slot], second_sem.at[slot])
        return total

    def send_last(dz):
        slot = dz - 1
        last_out[slot] = sum_second(dz).astype(last_out.dtype)
        copy_to(last_out.at[slot], last.at[slot], last_sent.at[slot], last_sem.at[slot], here.device(dz, 0, 0)).start()

    def step(turn, carry):
        layer, rest = turn // square, turn % square
        dz = (layer + 1) % deep
        following = (layer + 2) % deep
        i, j = side - 1 - rest % side, side - 1 - rest // side

        theirs = here.mirror(dz, i, j)
        arrived(theirs)

        def give(slot, value):
            given[turn, slot] = value.astype(given.dtype)

        compute(theirs, give)
        copy_to(given.at[turn], mate.at[turn], given_sem.at[turn], mate_sem.at[turn], partner).start()

        mine = here.block(dz, i, j)

        def keep_fresh(slot, value):
            fresh[slot] = value

        compute(mine, keep_fresh)

        @pl.when((rest == 0) & (layer < deep - 2))
        def _():
            for step in range(1, side):
                pass_on(following, step, 0, to_third=True)

        @pl.when((rest == square - 2) & (layer < deep - 1))
        def _():
            for a in range(side):
                for b in range(1, side):
                    pass_on(following, a, b)

        @pl.when((rest == 0) & (layer > 0))
        def _():
            send_last(layer)

        fresh[...] = fresh[...] + take(mate.at[turn], mate_sem.at[turn])

        @pl.when(j > 0)
        def _():
            slot = third_slot(dz, i, j)
            third_out[slot] = fresh[...].astype(third_out.dtype)
            copy_to(third_out.at[slot], third.at[slot], third_sent.at[slot], third_sem.at[slot], here.device(0, 0, j)).start()

        @pl.when(j == 0)
        def _():
            held[dz * side + i] = fresh[...]
            total = sum_third(dz, i)
            held[dz * side + i] = total

            @pl.when(i > 0)
            def _():
                slot = dz * (side - 1) + i - 1
                second_out[slot] = total.astype(second_out.dtype)
                copy_to(second_out.at[slot], second.at[slot], second_sent.at[slot], second_sem.at[slot], here.device(0, i, 0)).start()

        return carry

    lax.fori_loop(0, deep * square, step, 0)
    total = sum_second(0)
    for dz in range(1, deep):
        total = total + take(last.at[dz - 1], last_sem.at[dz - 1])
    out_ref[...] = total

    for sems in (fan_sem, hop3_sem, hop2_sem, hopz_sem, given_sem, third_sent, second_sent, last_sent):
        def drain(turn, carry, sems=sems):
            copy_to(given.at[0], mate.at[0], sems.at[turn], mate_sem.at[0], partner).wait_send()
            return carry

        lax.fori_loop(0, sems.shape[0], drain, 0)


def residual_parts(ints_ac, slot_pair, own, pairs, aux):
    blocks = pairs * aux
    deep, side, _ = layout_of(pairs, aux)
    local, width, lanes = own.shape
    count, funcs, _ = ints_ac.shape
    thirds, seconds, lasts = deep * side * (side - 1), deep * (side - 1), deep - 1

    def buffers(number, kind=own.dtype):
        return pltpu.VMEM((number,) + own.shape, kind)

    dma = pltpu.SemaphoreType.DMA
    return pl.pallas_call(
        functools.partial(residual_kernel, pairs, aux),
        in_specs=[
            pl.BlockSpec(memory_space=pltpu.SMEM),
            pl.BlockSpec(memory_space=pl.ANY),
            pl.BlockSpec(memory_space=pltpu.VMEM),
        ],
        out_specs=pl.BlockSpec(memory_space=pltpu.VMEM),
        out_shape=jax.ShapeDtypeStruct(own.shape, jnp.float32),
        scratch_shapes=[
            pltpu.VMEM(ints_ac.shape, ints_ac.dtype),
            buffers(blocks),
            pltpu.VMEM((local, funcs * width // 2, lanes), jnp.float32),
            pltpu.VMEM(own.shape, jnp.float32),
            buffers(blocks // 2),
            buffers(blocks // 2),
            buffers(deep * side, jnp.float32),
            buffers(thirds),
            buffers(thirds),
            buffers(seconds),
            buffers(seconds),
            buffers(lasts),
            buffers(lasts),
            dma((CHUNKS,)),
            dma,
            dma((blocks,)),
            dma((blocks // 2,)),
            dma((thirds,)),
            dma((seconds,)),
            dma((lasts,)),
            dma((blocks // 2,)),
            dma((blocks // 2,)),
            dma((thirds,)),
            dma((thirds,)),
            dma((seconds,)),
            dma((seconds,)),
            dma((lasts,)),
            dma((lasts,)),
        ],
        compiler_params=pltpu.CompilerParams(collective_id=0, has_side_effects=True, vmem_limit_bytes=62 << 20),
        name="residual_parts",
    )(slot_pair, ints_ac, own)


def body(pairs, aux, ints_ac, slot_pair, amplitudes, ranks, pair_occ, pno_energy, occ_energy):
    width = pno_energy.shape[1]
    local = amplitudes.shape[0]
    positions = jnp.arange(width, dtype=jnp.int32)
    masks = (positions[None, :] < ranks[:, None]).astype(jnp.float32)
    square = masks[:, :, None] * masks[:, None, :]
    masked_t = amplitudes.astype(jnp.float32).reshape(local, 2, width, width) * square[:, None]
    own = masked_t.astype(jnp.bfloat16).transpose(0, 2, 1, 3).reshape(local, width, 2 * width)
    summed = residual_parts(ints_ac, slot_pair, own, pairs, aux)
    source = (positions % 2) * (width // 2) + positions // 2
    place = (positions[:, None] == source[None, :]).astype(jnp.float32)
    split = summed.reshape(local, width, 2, width)
    residual = jnp.einsum(
        "jykx,xa,yb->jkab", split, place, place, precision=lax.Precision.HIGHEST
    )
    residual = residual * square[:, None]
    onehot = (
        pair_occ[:, :, None] == jnp.arange(occ_energy.shape[0], dtype=jnp.int32)[None, None, :]
    ).astype(jnp.float32)
    occ_pair = jnp.einsum("jko,o->jk", onehot, occ_energy, precision=lax.Precision.HIGHEST)
    denom = (
        pno_energy[:, :, None]
        + pno_energy[:, None, :]
        - (occ_pair[:, 0] + occ_pair[:, 1])[:, None, None]
    )
    updated = (masked_t - residual / denom[:, None]) * square[:, None]
    return (
        residual.reshape(local, 2, width * width),
        updated.reshape(local, 2, width * width).astype(jnp.bfloat16),
    )


def solution(mesh):
    placed = (
        P(None, ("pair", "aux"), None),
        P(),
        P(("pair", "aux"), None, None),
        P(("pair", "aux")),
        P(("pair", "aux"), None),
        P(("pair", "aux"), None),
        P(),
    )
    return jax.shard_map(
        functools.partial(body, mesh.shape["pair"], mesh.shape["aux"]),
        mesh=mesh,
        in_specs=placed,
        out_specs=(P(("pair", "aux"), None, None), P(("pair", "aux"), None, None)),
        check_vma=False,
    )
```

time: 211 us -> 78.8 us (0.37)
  waiting for transfers between devices: 133 us -> 0 us
  Pallas kernels: 47.9 us -> 68.7 us
  between operations: 14.1 us -> 0.7 us
  starting transfers between devices: 3.37 us -> 0 us
    all_to_all x1 -> x0, waiting for transfers between devices: 71.3 us -> none  [body(): parts = lax.all_to_all(out, ('pair', 'aux'), 0, 0, tiled=True)]
    all_gather x1 -> x0, waiting for transfers between devices: 62 us -> none  [body(): every = lax.all_gather(own, ('pair', 'aux'), axis=0, tiled=True)]
    pallas_call x1, Pallas kernels: 47.9 us -> 68.7 us  [residual_parts(): pl.pallas_call(functools.partial(residual_kernel, pairs, aux), in_specs=[...]
    all_to_all x1 -> x0, starting transfers between devices: 3.33 us -> none  [body(): parts = lax.all_to_all(out, ('pair', 'aux'), 0, 0, tiled=True)]
  transfers between devices with their start and end apart: 2 -> 0, of which waited for: 2 -> 0; matrix products, arithmetic and copies ran while one was open for 0% -> 0% of each run, Pallas kernels for 0% -> 0%
where the time goes in v2:
time: 78.8 us; the launch traced here: 77.8 us
  Pallas kernels  68.7 us (87%)
  local copies, waits for them, and re-layouts  5.62 us (7%)
  other arithmetic  1.86 us (2%)
  matrix products  0.84 us (1%)
    pallas_call x1, Pallas kernels, residual_parts(): pl.pallas_call(functools.partial(residual_kernel, pairs, aux), in_specs=[...  68.7 us

profile of v2, /device:TPU:0, one launch (start us, length us, event | category | flops | bytes accessed | tf_op | source)
XLA Modules:
  0.0 77.8 jit_solution(12814666437563087173)
XLA Ops:
  0.6 0.0 copy-start
  0.7 0.7 fusion.10
  1.4 0.8 copy.10
  2.1 0.1 iota_compare_fusion.1
  2.2 0.0 copy-done
  2.2 0.1 fusion.8
  2.4 1.0 %add_subtract_fusion = (f32[6,64,64]{2,1,0:T(8,128)S(1)}, f32[6,64,64]{2,1,0:T(8,128)S(1)}) fusion(f32[6]{0:T(128)S(1)} %add_bitcast_fusion, f32[6,64]{1,0:T(8,128)} %param.12, f32[6,64]{1,0:T(8,128)S(1)} %fusion.10), kind=kLoop, calls=%fused_computation.5 | loop fusion | flops 73728 | bytes 199704 | tf_op jit(solution)/shard_map/sub | solution.py:369
  3.4 1.0 %reshape.103 = f32[6,2,64,64]{3,2,1,0:T(8,128)S(1)} reshape(bf16[6,2,4096]{2,1,0:T(2,128)(2,1)} %param.9) | data formatting | bytes 294912 | tf_op jit(solution)/shard_map/reshape | solution.py:354
  4.5 0.2 copy.9
  4.7 0.8 %reshape.99.own_ref = bf16[6,64,128]{2,1,0:T(8,128)(2,1)} reshape(bf16[6,64,2,64]{3,2,1,0:T(2,128)(2,1)S(1)} %copy.9) | data formatting | bytes 196608 | tf_op jit(solution)/shard_map/reshape | solution.py:355
  5.5 68.7 %residual_parts.1 = f32[6,64,128]{2,1,0:T(8,128)} custom-call(s32[192]{0:T(256)} %order_ref.1, bf16[192,16,4096]{2,1,0:T(8,128)(2,1)} %ints_ref.1, bf16[6,64,128]{2,1,0:T(8,128)(2,1)} %reshape.99.own_ref), custom_call_target="tpu_custom_call" | custom-call | tf_op jit(solution)/shard_map/residual_parts/pallas_call | solution.py:304
  74.2 1.1 %copy.15 = f32[6,64,128]{1,2,0:T(8,128)S(1)} copy(f32[6,64,128]{2,1,0:T(8,128)} %residual_parts.1) | data formatting | bytes 393216 | tf_op jit(solution)/shard_map/reshape | solution.py:359
  75.3 0.4 fusion.4
  75.7 0.3 multiply_convert_fusion
  76.0 0.8 %convert_element_type.26 = bf16[6,2,4096]{2,1,0:T(2,128)(2,1)} reshape(bf16[6,2,64,64]{3,2,1,0:T(8,128)(2,1)S(1)} %get-tuple-element.2) | data formatting | bytes 196608 | tf_op jit(solution)/shard_map/convert_element_type | solution.py:376
  76.9 0.9 %reshape.101 = f32[6,2,4096]{2,1,0:T(2,128)} reshape(f32[6,2,64,64]{3,2,1,0:T(8,128)S(1)} %get-tuple-element.3) | data formatting | bytes 393216 | tf_op jit(solution)/shard_map/reshape | solution.py:375
  (3 shorter events, 0.1 us)
Async XLA Ops:
  0.6 1.6 %copy-start = (f32[48]{0:T(128)S(1)}, f32[48]{0:T(128)}, u32[]{:S(2)}) copy-start(f32[48]{0:T(128)} %param.13) | copy-start | bytes 580

commit v3 on v2

--- a/solution.py
+++ b/solution.py
@@ -8,51 +8,53 @@
 from jax.sharding import PartitionSpec as P
 
 CHUNKS = 8
-
-
-def exchange(load, amps, rows_ref):
-    width, lanes = amps.shape
+GAP = 4
+LAG = 4
+
+
+def spread(load, rows_ref, aux, width):
+    lanes = 2 * width
     chunks = width * width // lanes
-    aux = rows_ref.shape[0] // chunks
-    half_t = lax.broadcasted_iota(jnp.int32, (width, lanes), 1) < width
-    half_b = lax.broadcasted_iota(jnp.int32, (chunks, lanes), 1) < width
+    stride = aux + GAP
+    half = lax.broadcasted_iota(jnp.int32, (chunks, lanes), 1) < width
     for chunk in range(chunks):
-        rows_ref[pl.ds(chunk * aux, aux), :] = load(chunk).astype(jnp.float32)
+        rows_ref[pl.ds(chunk * stride, aux), :] = load(chunk).astype(jnp.float32)
     pieces = []
     for pair in range(aux // 2):
-        first = rows_ref[pl.ds(2 * pair, chunks, stride=aux), :]
-        second = rows_ref[pl.ds(2 * pair + 1, chunks, stride=aux), :]
-        crossed = pltpu.roll(jnp.where(half_b, second, first), width, 1)
-        even = jnp.where(half_b, first, crossed)
-        odd = jnp.where(half_b, crossed, second)
+        first = rows_ref[pl.ds(2 * pair, chunks, stride=stride), :]
+        second = rows_ref[pl.ds(2 * pair + 1, chunks, stride=stride), :]
+        crossed = pltpu.roll(jnp.where(half, second, first), width, 1)
+        even = jnp.where(half, first, crossed)
+        odd = jnp.where(half, crossed, second)
         pieces.append(jnp.concatenate([even, odd], axis=0).astype(jnp.bfloat16))
-    stacked = jnp.concatenate(pieces, axis=0)
+    return pieces
+
+
+def contract(pieces, amps):
+    width, lanes = amps.shape
+    half = lax.broadcasted_iota(jnp.int32, (width, lanes), 1) < width
     amps = amps.astype(jnp.float32)
     turned = pltpu.roll(amps, width, 1)
     none = jnp.zeros_like(amps)
     weights = jnp.concatenate(
         [
-            jnp.concatenate([jnp.where(half_t, amps, none), jnp.where(half_t, none, turned)], axis=0),
-            jnp.concatenate([jnp.where(half_t, turned, none), jnp.where(half_t, none, amps)], axis=0),
+            jnp.concatenate([jnp.where(half, amps, none), jnp.where(half, none, turned)], axis=0),
+            jnp.concatenate([jnp.where(half, turned, none), jnp.where(half, none, amps)], axis=0),
         ],
         axis=1,
     ).astype(jnp.bfloat16)
-    inner = jnp.dot(stacked, weights, preferred_element_type=jnp.float32).astype(jnp.bfloat16)
+    stacked = jnp.concatenate(pieces, axis=0)
+    return jnp.dot(stacked, weights, preferred_element_type=jnp.float32).astype(jnp.bfloat16)
+
+
+def close(pieces, inner):
+    width, lanes = pieces[0].shape
     left = jnp.concatenate(pieces, axis=1)
-    right = jnp.concatenate(
-        [
-            jnp.concatenate(
-                [
-                    inner[pair * width : (pair + 1) * width, k * lanes : (k + 1) * lanes]
-                    for pair in range(aux // 2)
-                ],
-                axis=1,
-            )
-            for k in range(2)
-        ],
-        axis=0,
-    )
-    return lax.dot_general(left, right, (((1,), (1,)), ((), ())), preferred_element_type=jnp.float32)
+    right = []
+    for index in range(len(pieces)):
+        rows = slice(index * width, (index + 1) * width)
+        right.append(jnp.concatenate([inner[rows, :lanes], inner[rows, lanes:]], axis=0).T)
+    return jnp.dot(left, jnp.concatenate(right, axis=0), preferred_element_type=jnp.float32)
 
 
 def layout_of(pairs, aux):
@@ -181,12 +183,23 @@
     for load in loads():
         load.wait()
 
-    def compute(block, store):
-        for slot in range(local):
+    def compute(jobs):
+        waiting = []
+
+        def finish():
+            store, pieces, inner = waiting.pop(0)
+            store(close(pieces, inner))
+
+        for job, (block, slot, store) in enumerate(jobs):
             pair = order_ref[block * local + slot]
-            store(slot, exchange(
-                lambda chunk: ints[pair, :, pl.ds(chunk * lanes, lanes)], amps[block, slot], rows.at[slot]
-            ))
+            pieces = spread(
+                lambda chunk: ints[pair, :, pl.ds(chunk * lanes, lanes)], rows.at[job], ints.shape[1], lanes // 2
+            )
+            waiting.append((store, pieces, contract(pieces, amps[block, slot])))
+            if len(waiting) > LAG:
+                finish()
+        while waiting:
+            finish()
 
     def as_float(value):
         return value.astype(jnp.float32)
@@ -197,13 +210,6 @@
 
     def third_slot(dz, i, j):
         return (dz * side + i) * (side - 1) + j - 1
-
-    def sum_third(dz, i):
-        total = held[dz * side + i]
-        for j in range(1, side):
-            slot = third_slot(dz, i, j)
-            total = total + take(third.at[slot], third_sem.at[slot])
-        return total
 
     def sum_second(dz):
         total = held[dz * side]
@@ -217,32 +223,65 @@
         last_out[slot] = sum_second(dz).astype(last_out.dtype)
         copy_to(last_out.at[slot], last.at[slot], last_sent.at[slot], last_sem.at[slot], here.device(dz, 0, 0)).start()
 
+    def shift_of(turn):
+        layer, rest = turn // square, turn % square
+        return (layer + 1) % deep, side - 1 - rest % side, side - 1 - rest // side
+
+    def settle(turn):
+        dz, i, j = shift_of(turn)
+        total = fresh[turn % 2] + take(mate.at[turn], mate_sem.at[turn])
+
+        @pl.when(j > 0)
+        def _():
+            slot = third_slot(dz, i, j)
+            third_out[slot] = total.astype(third_out.dtype)
+            copy_to(third_out.at[slot], third.at[slot], third_sent.at[slot], third_sem.at[slot], here.device(0, 0, j)).start()
+
+        @pl.when(j == 0)
+        def _():
+            whole = total
+            for other in range(1, side):
+                slot = third_slot(dz, i, other)
+                whole = whole + take(third.at[slot], third_sem.at[slot])
+            held[dz * side + i] = whole
+
+            @pl.when(i > 0)
+            def _():
+                slot = dz * (side - 1) + i - 1
+                second_out[slot] = whole.astype(second_out.dtype)
+                copy_to(second_out.at[slot], second.at[slot], second_sent.at[slot], second_sem.at[slot], here.device(0, i, 0)).start()
+
+    turns = deep * square
+
     def step(turn, carry):
         layer, rest = turn // square, turn % square
-        dz = (layer + 1) % deep
+        dz, i, j = shift_of(turn)
         following = (layer + 2) % deep
-        i, j = side - 1 - rest % side, side - 1 - rest // side
-
-        theirs = here.mirror(dz, i, j)
+        theirs, mine = here.mirror(dz, i, j), here.block(dz, i, j)
         arrived(theirs)
 
-        def give(slot, value):
-            given[turn, slot] = value.astype(given.dtype)
-
-        compute(theirs, give)
+        def give(slot):
+            def store(value):
+                given[turn, slot] = value.astype(given.dtype)
+
+            return store
+
+        def retain(slot):
+            def store(value):
+                fresh[turn % 2, slot] = value
+
+            return store
+
+        compute(
+            [(theirs, slot, give(slot)) for slot in range(local)]
+            + [(mine, slot, retain(slot)) for slot in range(local)]
+        )
         copy_to(given.at[turn], mate.at[turn], given_sem.at[turn], mate_sem.at[turn], partner).start()
 
-        mine = here.block(dz, i, j)
-
-        def keep_fresh(slot, value):
-            fresh[slot] = value
-
-        compute(mine, keep_fresh)
-
         @pl.when((rest == 0) & (layer < deep - 2))
         def _():
-            for step in range(1, side):
-                pass_on(following, step, 0, to_third=True)
+            for hop in range(1, side):
+                pass_on(following, hop, 0, to_third=True)
 
         @pl.when((rest == square - 2) & (layer < deep - 1))
         def _():
@@ -250,33 +289,18 @@
                 for b in range(1, side):
                     pass_on(following, a, b)
 
-        @pl.when((rest == 0) & (layer > 0))
+        @pl.when(turn > 0)
+        def _():
+            settle(turn - 1)
+
+        @pl.when((rest == 1) & (layer > 0))
         def _():
             send_last(layer)
 
-        fresh[...] = fresh[...] + take(mate.at[turn], mate_sem.at[turn])
-
-        @pl.when(j > 0)
-        def _():
-            slot = third_slot(dz, i, j)
-            third_out[slot] = fresh[...].astype(third_out.dtype)
-            copy_to(third_out.at[slot], third.at[slot], third_sent.at[slot], third_sem.at[slot], here.device(0, 0, j)).start()
-
-        @pl.when(j == 0)
-        def _():
-            held[dz * side + i] = fresh[...]
-            total = sum_third(dz, i)
-            held[dz * side + i] = total
-
-            @pl.when(i > 0)
-            def _():
-                slot = dz * (side - 1) + i - 1
-                second_out[slot] = total.astype(second_out.dtype)
-                copy_to(second_out.at[slot], second.at[slot], second_sent.at[slot], second_sem.at[slot], here.device(0, i, 0)).start()
-
         return carry
 
-    lax.fori_loop(0, deep * square, step, 0)
+    lax.fori_loop(0, turns, step, 0)
+    settle(turns - 1)
     total = sum_second(0)
     for dz in range(1, deep):
         total = total + take(last.at[dz - 1], last_sem.at[dz - 1])
@@ -313,8 +337,8 @@
         scratch_shapes=[
             pltpu.VMEM(ints_ac.shape, ints_ac.dtype),
             buffers(blocks),
-            pltpu.VMEM((local, funcs * width // 2, lanes), jnp.float32),
-            pltpu.VMEM(own.shape, jnp.float32),
+            pltpu.VMEM((2 * local, (width // 2 + 1) * (funcs + GAP), lanes), jnp.float32),
+            buffers(2, jnp.float32),
             buffers(blocks // 2),
             buffers(blocks // 2),
             buffers(deep * side, jnp.float32),

time: 78.8 us -> 64.8 us (0.82)
  Pallas kernels: 68.7 us -> 54.6 us
    pallas_call x1, Pallas kernels: 68.7 us -> 54.6 us  [residual_parts(): pl.pallas_call(functools.partial(residual_kernel, pairs, aux), in_specs=[...]
where the time goes in v3:
time: 64.8 us; the launch traced here: 63.7 us
  Pallas kernels  54.6 us (84%)
  local copies, waits for them, and re-layouts  5.62 us (9%)
  other arithmetic  1.86 us (3%)
  matrix products  0.84 us (1%)
  between operations  0.7 us (1%)
    pallas_call x1, Pallas kernels, residual_parts(): pl.pallas_call(functools.partial(residual_kernel, pairs, aux), in_specs=[...  54.6 us

profile of v3, /device:TPU:0, one launch (start us, length us, event | category | flops | bytes accessed | tf_op | source)
XLA Modules:
  0.0 63.7 jit_solution(5104255430862008121)
XLA Ops:
  0.6 0.0 copy-start
  0.7 0.7 %fusion.10 = f32[6,64]{1,0:T(8,128)S(1)} fusion(s32[6]{0:T(128)} %param.10), kind=kLoop, calls=%fused_computation.16 | loop fusion | flops 768 | bytes 1560 | tf_op jit(solution)/shard_map/convert_element_type | solution.py:376
  1.4 0.8 %copy.10 = s32[6,2]{1,0:T(8,128)S(1)} copy(s32[6,2]{0,1:T(2,128)} %param.11) | data formatting | bytes 96 | tf_op args[4]
  2.1 0.1 iota_compare_fusion.1
  2.2 0.0 copy-done
  2.2 0.1 fusion.8
  2.4 1.0 %add_subtract_fusion = (f32[6,64,64]{2,1,0:T(8,128)S(1)}, f32[6,64,64]{2,1,0:T(8,128)S(1)}) fusion(f32[6]{0:T(128)S(1)} %add_bitcast_fusion, f32[6,64]{1,0:T(8,128)} %param.12, f32[6,64]{1,0:T(8,128)S(1)} %fusion.10), kind=kLoop, calls=%fused_computation.5 | loop fusion | flops 73728 | bytes 199704 | tf_op jit(solution)/shard_map/sub | solution.py:393
  3.4 1.0 %reshape.103 = f32[6,2,64,64]{3,2,1,0:T(8,128)S(1)} reshape(bf16[6,2,4096]{2,1,0:T(2,128)(2,1)} %param.9) | data formatting | bytes 294912 | tf_op jit(solution)/shard_map/reshape | solution.py:378
  4.5 0.2 copy.9
  4.7 0.8 %reshape.99.own_ref = bf16[6,64,128]{2,1,0:T(8,128)(2,1)} reshape(bf16[6,64,2,64]{3,2,1,0:T(2,128)(2,1)S(1)} %copy.9) | data formatting | bytes 196608 | tf_op jit(solution)/shard_map/reshape | solution.py:379
  5.5 54.6 %residual_parts.1 = f32[6,64,128]{2,1,0:T(8,128)} custom-call(s32[192]{0:T(256)} %order_ref.1, bf16[192,16,4096]{2,1,0:T(8,128)(2,1)} %ints_ref.1, bf16[6,64,128]{2,1,0:T(8,128)(2,1)} %reshape.99.own_ref), custom_call_target="tpu_custom_call" | custom-call | tf_op jit(solution)/shard_map/residual_parts/pallas_call | solution.py:328
  60.1 1.1 %copy.15 = f32[6,64,128]{1,2,0:T(8,128)S(1)} copy(f32[6,64,128]{2,1,0:T(8,128)} %residual_parts.1) | data formatting | bytes 393216 | tf_op jit(solution)/shard_map/reshape | solution.py:383
  61.2 0.4 fusion.4
  61.6 0.3 multiply_convert_fusion
  61.9 0.8 %convert_element_type.26 = bf16[6,2,4096]{2,1,0:T(2,128)(2,1)} reshape(bf16[6,2,64,64]{3,2,1,0:T(8,128)(2,1)S(1)} %get-tuple-element.2) | data formatting | bytes 196608 | tf_op jit(solution)/shard_map/convert_element_type | solution.py:400
  62.8 0.9 %reshape.101 = f32[6,2,4096]{2,1,0:T(2,128)} reshape(f32[6,2,64,64]{3,2,1,0:T(8,128)S(1)} %get-tuple-element.3) | data formatting | bytes 393216 | tf_op jit(solution)/shard_map/reshape | solution.py:399
  (3 shorter events, 0.1 us)
Async XLA Ops:
  0.6 1.6 %copy-start = (f32[48]{0:T(128)S(1)}, f32[48]{0:T(128)}, u32[]{:S(2)}) copy-start(f32[48]{0:T(128)} %param.13) | copy-start | bytes 580

commit v4 on v3

--- a/solution.py
+++ b/solution.py
@@ -1,4 +1,5 @@
 import functools
+import math
 
 import jax
 import jax.numpy as jnp
@@ -118,15 +119,15 @@
 
 
 def residual_kernel(
-    pairs, aux, order_ref, ints_ref, own_ref, out_ref,
-    ints, amps, rows, fresh, given, mate, held, third, third_out, second, second_out, last, last_out,
-    ints_sem, keep_sem, recv_sem, fan_sem, hop3_sem, hop2_sem, hopz_sem,
+    pairs, aux, order_ref, ranks_ref, ints_ref, raw_ref, out_ref,
+    ints, amps, plain, rows, fresh, given, mate, held, third, third_out, second, second_out, last, last_out,
+    ints_sem, recv_sem, fan_sem, hop3_sem, hop2_sem, hopz_sem,
     given_sem, mate_sem, third_sent, third_sem, second_sent, second_sem, last_sent, last_sem,
 ):
     here = Place(pairs, aux)
     deep, side = here.deep, here.side
-    local = own_ref.shape[0]
-    lanes = own_ref.shape[2]
+    local, width, lanes = out_ref.shape
+    home = amps.at[here.block(0, 0, 0)]
     partner = here.partner()
     square = side * side
     count = ints.shape[0]
@@ -139,14 +140,24 @@
 
     for load in loads():
         load.start()
-    keep = pltpu.make_async_copy(own_ref, amps.at[here.block(0, 0, 0)], keep_sem)
-    keep.start()
+    for slot in range(local):
+        natural(raw_ref, slot, plain.at[0])
+        half = width // 2
+        zero, one = plain[0, :half], plain[0, half:]
+        low = lax.broadcasted_iota(jnp.int32, (half, lanes), 1) < width
+        crossed = pltpu.roll(jnp.where(low, one, zero), width, 1)
+        plain[1, pl.ds(0, half, stride=2), :] = jnp.where(low, zero, crossed)
+        plain[1, pl.ds(1, half, stride=2), :] = jnp.where(low, crossed, one)
+        row = lax.broadcasted_iota(jnp.int32, (width, lanes), 0)
+        column = lax.broadcasted_iota(jnp.int32, (width, lanes), 1) % width
+        inside = (row < ranks_ref[slot]) & (column < ranks_ref[slot])
+        home[slot] = jnp.where(inside, plain[1], 0.0).astype(home.dtype)
     here.greet()
 
-    def forward(dz, i, j, source=None, to_third=False, to_second=False, to_deep=False):
+    def forward(dz, i, j, to_third=False, to_second=False, to_deep=False):
         block = here.block(dz, i, j)
         target, arrival = amps.at[block], recv_sem.at[block]
-        source = target if source is None else source
+        source = target
         family = (dz * side + i) * side + j
         if to_third:
             for step in range(1, side):
@@ -168,7 +179,7 @@
         arrived(here.block(dz, i, j))
         forward(dz, i, j, **where)
 
-    forward(0, 0, 0, own_ref, to_third=True, to_second=True, to_deep=True)
+    forward(0, 0, 0, to_third=True, to_second=True, to_deep=True)
     for i in range(1, side):
         pass_on(0, i, 0, to_third=True)
     pass_on(1, 0, 0, to_third=True, to_second=True)
@@ -179,7 +190,6 @@
     for i in range(side):
         for j in range(1, side):
             pass_on(1, i, j)
-    keep.wait()
     for load in loads():
         load.wait()
 
@@ -314,29 +324,34 @@
         lax.fori_loop(0, sems.shape[0], drain, 0)
 
 
-def residual_parts(ints_ac, slot_pair, own, pairs, aux):
+def residual_parts(ints_ac, slot_pair, amplitudes, ranks, pairs, aux):
     blocks = pairs * aux
     deep, side, _ = layout_of(pairs, aux)
-    local, width, lanes = own.shape
-    count, funcs, _ = ints_ac.shape
+    count, funcs, size = ints_ac.shape
+    width = math.isqrt(size)
+    lanes = 2 * width
+    local = amplitudes.shape[0]
+    shape = (local, width, lanes)
     thirds, seconds, lasts = deep * side * (side - 1), deep * (side - 1), deep - 1
 
-    def buffers(number, kind=own.dtype):
-        return pltpu.VMEM((number,) + own.shape, kind)
+    def buffers(number, kind=amplitudes.dtype):
+        return pltpu.VMEM((number,) + shape, kind)
 
     dma = pltpu.SemaphoreType.DMA
     return pl.pallas_call(
         functools.partial(residual_kernel, pairs, aux),
         in_specs=[
             pl.BlockSpec(memory_space=pltpu.SMEM),
+            pl.BlockSpec(memory_space=pltpu.SMEM),
             pl.BlockSpec(memory_space=pl.ANY),
             pl.BlockSpec(memory_space=pltpu.VMEM),
         ],
         out_specs=pl.BlockSpec(memory_space=pltpu.VMEM),
-        out_shape=jax.ShapeDtypeStruct(own.shape, jnp.float32),
+        out_shape=jax.ShapeDtypeStruct(shape, jnp.float32),
         scratch_shapes=[
             pltpu.VMEM(ints_ac.shape, ints_ac.dtype),
             buffers(blocks),
+            pltpu.VMEM((2, width, lanes), jnp.float32),
             pltpu.VMEM((2 * local, (width // 2 + 1) * (funcs + GAP), lanes), jnp.float32),
             buffers(2, jnp.float32),
             buffers(blocks // 2),
@@ -349,7 +364,6 @@
             buffers(lasts),
             buffers(lasts),
             dma((CHUNKS,)),
-            dma,
             dma((blocks,)),
             dma((blocks // 2,)),
             dma((thirds,)),
@@ -366,39 +380,68 @@
         ],
         compiler_params=pltpu.CompilerParams(collective_id=0, has_side_effects=True, vmem_limit_bytes=62 << 20),
         name="residual_parts",
-    )(slot_pair, ints_ac, own)
+    )(slot_pair, ranks, ints_ac, amplitudes)
+
+
+def natural(raw_ref, slot, target):
+    half, lanes = target.shape[0] // 2, target.shape[1]
+    for chunk in range(half):
+        target[pl.ds(chunk, 2, stride=half), :] = raw_ref[slot, :, pl.ds(chunk * lanes, lanes)].astype(jnp.float32)
+
+
+def update_kernel(
+    ranks_ref, pair_ref, occ_ref, sum_ref, raw_ref, energy_ref, residual_ref, new_ref, plain, turned, column, packed
+):
+    local, width, lanes = sum_ref.shape
+    half = width // 2
+    low = lax.broadcasted_iota(jnp.int32, (half, lanes), 1) < width
+    lane = lax.broadcasted_iota(jnp.int32, (half, lanes), 1)
+    a = 2 * lax.broadcasted_iota(jnp.int32, (half, lanes), 0) + lane // width
+    b = lane % width
+    for slot in range(local):
+        natural(raw_ref, slot, plain.at[slot])
+        turned[slot, pl.ds(0, half, stride=2), :] = sum_ref[slot, :half]
+        turned[slot, pl.ds(1, half, stride=2), :] = sum_ref[slot, half:]
+        flipped = turned[slot].T
+        energy = energy_ref[pl.ds(slot, 1), :]
+        along = jnp.concatenate([energy, energy], axis=1)
+        column[slot] = jnp.broadcast_to(along, (lanes, lanes)).T
+        down = jnp.where(low, column[slot, pl.ds(0, half, stride=2), :], column[slot, pl.ds(1, half, stride=2), :])
+        occupied = occ_ref[pair_ref[slot, 0]] + occ_ref[pair_ref[slot, 1]]
+        denom = down + along - occupied
+        inside = (a < ranks_ref[slot]) & (b < ranks_ref[slot])
+        for k in range(2):
+            block = flipped[k * width : (k + 1) * width]
+            residual = jnp.where(inside, jnp.concatenate([block[:half], block[half:]], axis=1), 0.0)
+            kept = jnp.where(inside, plain[slot, k * half : (k + 1) * half], 0.0)
+            packed[slot, 0, k * half : (k + 1) * half] = residual
+            packed[slot, 1, k * half : (k + 1) * half] = jnp.where(inside, kept - residual / denom, 0.0)
+        for chunk in range(half):
+            span = pl.ds(chunk * lanes, lanes)
+            residual_ref[slot, :, span] = packed[slot, 0, pl.ds(chunk, 2, stride=half), :]
+            new_ref[slot, :, span] = packed[slot, 1, pl.ds(chunk, 2, stride=half), :].astype(new_ref.dtype)
 
 
 def body(pairs, aux, ints_ac, slot_pair, amplitudes, ranks, pair_occ, pno_energy, occ_energy):
-    width = pno_energy.shape[1]
-    local = amplitudes.shape[0]
-    positions = jnp.arange(width, dtype=jnp.int32)
-    masks = (positions[None, :] < ranks[:, None]).astype(jnp.float32)
-    square = masks[:, :, None] * masks[:, None, :]
-    masked_t = amplitudes.astype(jnp.float32).reshape(local, 2, width, width) * square[:, None]
-    own = masked_t.astype(jnp.bfloat16).transpose(0, 2, 1, 3).reshape(local, width, 2 * width)
-    summed = residual_parts(ints_ac, slot_pair, own, pairs, aux)
-    source = (positions % 2) * (width // 2) + positions // 2
-    place = (positions[:, None] == source[None, :]).astype(jnp.float32)
-    split = summed.reshape(local, width, 2, width)
-    residual = jnp.einsum(
-        "jykx,xa,yb->jkab", split, place, place, precision=lax.Precision.HIGHEST
-    )
-    residual = residual * square[:, None]
-    onehot = (
-        pair_occ[:, :, None] == jnp.arange(occ_energy.shape[0], dtype=jnp.int32)[None, None, :]
-    ).astype(jnp.float32)
-    occ_pair = jnp.einsum("jko,o->jk", onehot, occ_energy, precision=lax.Precision.HIGHEST)
-    denom = (
-        pno_energy[:, :, None]
-        + pno_energy[:, None, :]
-        - (occ_pair[:, 0] + occ_pair[:, 1])[:, None, None]
-    )
-    updated = (masked_t - residual / denom[:, None]) * square[:, None]
-    return (
-        residual.reshape(local, 2, width * width),
-        updated.reshape(local, 2, width * width).astype(jnp.bfloat16),
-    )
+    summed = residual_parts(ints_ac, slot_pair, amplitudes, ranks, pairs, aux)
+    local, width, lanes = summed.shape
+    smem, vmem = pl.BlockSpec(memory_space=pltpu.SMEM), pl.BlockSpec(memory_space=pltpu.VMEM)
+    return pl.pallas_call(
+        update_kernel,
+        in_specs=[smem, smem, smem, vmem, vmem, vmem],
+        out_specs=(vmem, vmem),
+        out_shape=(
+            jax.ShapeDtypeStruct(amplitudes.shape, jnp.float32),
+            jax.ShapeDtypeStruct(amplitudes.shape, amplitudes.dtype),
+        ),
+        scratch_shapes=[
+            pltpu.VMEM((local, width, lanes), jnp.float32),
+            pltpu.VMEM((local, width, lanes), jnp.float32),
+            pltpu.VMEM((local, lanes, lanes), jnp.float32),
+            pltpu.VMEM((local, 2, width, lanes), jnp.float32),
+        ],
+        name="update",
+    )(ranks, pair_occ, occ_energy, summed, amplitudes, pno_energy)
 
 
 def solution(mesh):

time: 64.8 us -> 60 us (0.926)
  local copies, waits for them, and re-layouts: 5.62 us -> 1.34 us
  Pallas kernels: 54.6 us -> 57 us
  other arithmetic: 1.86 us -> 0 us
  matrix products: 0.84 us -> 0 us
    reshape x4 -> x0, local copies, waits for them, and re-layouts: 3.8 us -> none  [the longest x1 1.09 us: body(): split = summed.reshape(local, width, 2, width)]
    pallas_call x0 -> x1, Pallas kernels: none -> 2.45 us  [body(): pl.pallas_call(update_kernel, in_specs=[smem, smem, smem, vmem, vmem, vme...]
    sub x1 -> x0, other arithmetic: 1 us -> none  [body(): pno_energy[:, :, None] + pno_energy[:, None, :]]
    convert_element_type x1 -> x0, local copies, waits for them, and re-layouts: 0.85 us -> none  [body(): updated.reshape(local, 2, width * width).astype(jnp.bfloat16)]
    dot_general x3 -> x0, matrix products: 0.84 us -> none  [the longest x2 0.71 us: body(): jnp.einsum('jykx,xa,yb->jkab', split, place, place, precision=lax.Precisi...]
    convert_element_type x1 -> x0, other arithmetic: 0.73 us -> none  [body(): masks = (positions[None, :] < ranks[:, None]).astype(jnp.float32)]
    unnamed x3 -> x1, local copies, waits for them, and re-layouts: 0.77 us -> 1.34 us
where the time goes in v4:
time: 60 us; the launch traced here: 59 us
  Pallas kernels  57 us (95%)
  local copies, waits for them, and re-layouts  1.34 us (2%)
  between operations  0.64 us (1%)
    pallas_call x1, Pallas kernels, residual_parts(): pl.pallas_call(functools.partial(residual_kernel, pairs, aux), in_specs=[...  54.6 us
    pallas_call x1, Pallas kernels, body(): pl.pallas_call(update_kernel, in_specs=[smem, smem, smem, vmem, vmem, vme...  2.45 us
    unnamed x1, local copies, waits for them, and re-layouts  1.34 us

profile of v4, /device:TPU:0, one launch (start us, length us, event | category | flops | bytes accessed | tf_op | source)
XLA Modules:
  0.0 59.0 jit_solution(8380389288549091769)
XLA Ops:
  0.6 1.3 %copy.9.pair_ref = s32[6,2]{1,0:T(8,128)} copy(s32[6,2]{0,1:T(2,128)} %param.11) | data formatting | bytes 96 | tf_op args[4]
  2.0 54.6 %residual_parts.1.sum_ref = f32[6,64,128]{2,1,0:T(8,128)} custom-call(s32[192]{0:T(256)} %order_ref.1, s32[6]{0:T(128)} %ranks_ref.3, bf16[192,16,4096]{2,1,0:T(8,128)(2,1)} %ints_ref.1, bf16[6,2,4096]{2,1,0:T(2,128)(2,1)} %raw_ref.3), custom_call_target="tpu_custom_call" | custom-call | tf_op jit(solution)/shard_map/residual_parts/pallas_call | solution.py:341
  56.6 2.5 %update.1 = (f32[6,2,4096]{2,1,0:T(2,128)}, bf16[6,2,4096]{2,1,0:T(2,128)(2,1)}) custom-call(s32[6]{0:T(128)} %ranks_ref.3, s32[6,2]{1,0:T(8,128)} %copy.9.pair_ref, f32[48]{0:T(128)} %occ_ref.1, f32[6,64,128]{2,1,0:T(8,128)} %residual_parts.1.sum_ref, bf16[6,2,4096]{2,1,0:T(2,128)(2,1)} %raw_ref.3, f32[6,64]{1,0:T(8,128)} %energy_ref.1), custom_call_target="tpu_custom_call" | custom-call | tf_op jit(solution)/shard_map/update/pallas_call | solution.py:429

commit v5 on v4

--- a/solution.py
+++ b/solution.py
@@ -407,7 +407,7 @@
         along = jnp.concatenate([energy, energy], axis=1)
         column[slot] = jnp.broadcast_to(along, (lanes, lanes)).T
         down = jnp.where(low, column[slot, pl.ds(0, half, stride=2), :], column[slot, pl.ds(1, half, stride=2), :])
-        occupied = occ_ref[pair_ref[slot, 0]] + occ_ref[pair_ref[slot, 1]]
+        occupied = occ_ref[pair_ref[0, slot]] + occ_ref[pair_ref[1, slot]]
         denom = down + along - occupied
         inside = (a < ranks_ref[slot]) & (b < ranks_ref[slot])
         for k in range(2):
@@ -441,7 +441,7 @@
             pltpu.VMEM((local, 2, width, lanes), jnp.float32),
         ],
         name="update",
-    )(ranks, pair_occ, occ_energy, summed, amplitudes, pno_energy)
+    )(ranks, pair_occ.T, occ_energy, summed, amplitudes, pno_energy)
 
 
 def solution(mesh):

time: 60 us -> 58.6 us (0.977)
  local copies, waits for them, and re-layouts: 1.34 us -> 0 us
    unnamed x1 -> x0, local copies, waits for them, and re-layouts: 1.34 us -> none
where the time goes in v5:
time: 58.6 us; the launch traced here: 57.7 us
  Pallas kernels  57 us (97%)
  between operations  0.64 us (1%)
    pallas_call x1, Pallas kernels, residual_parts(): pl.pallas_call(functools.partial(residual_kernel, pairs, aux), in_specs=[...  54.6 us
    pallas_call x1, Pallas kernels, body(): pl.pallas_call(update_kernel, in_specs=[smem, smem, smem, vmem, vmem, vme...  2.45 us

profile of v5, /device:TPU:0, one launch (start us, length us, event | category | flops | bytes accessed | tf_op | source)
XLA Modules:
  0.0 57.7 jit_solution(12280952536860488311)
XLA Ops:
  0.6 54.6 %residual_parts.1.sum_ref = f32[6,64,128]{2,1,0:T(8,128)} custom-call(s32[192]{0:T(256)} %order_ref.1, s32[6]{0:T(128)} %ranks_ref.3, bf16[192,16,4096]{2,1,0:T(8,128)(2,1)} %ints_ref.1, bf16[6,2,4096]{2,1,0:T(2,128)(2,1)} %raw_ref.3), custom_call_target="tpu_custom_call" | custom-call | tf_op jit(solution)/shard_map/residual_parts/pallas_call | solution.py:341
  55.2 2.5 %update.1 = (f32[6,2,4096]{2,1,0:T(2,128)}, bf16[6,2,4096]{2,1,0:T(2,128)(2,1)}) custom-call(s32[6]{0:T(128)} %ranks_ref.3, s32[2,6]{1,0:T(2,128)} %bitcast.1, f32[48]{0:T(128)} %occ_ref.1, f32[6,64,128]{2,1,0:T(8,128)} %residual_parts.1.sum_ref, bf16[6,2,4096]{2,1,0:T(2,128)(2,1)} %raw_ref.3, f32[6,64]{1,0:T(8,128)} %energy_ref.1), custom_call_target="tpu_custom_call" | custom-call | tf_op jit(solution)/shard_map/update/pallas_call | solution.py:429
